TPU v7x, 32 devices: a whole 2x2x4 slice. The times are simulated.
32 devices in a mesh: ctx: 8 (over z, y), wt: 4 (over x, core).
Axes of the slice: x: 2, y: 2, z: 4, core: 2. Of those that a mesh axis runs over, the one named last changes fastest.
Arguments:
- tokens: bfloat16 [4, 2048, 2048], P('wt', 'ctx'), may hold values from -6 to 6
- out_grad: bfloat16 [4, 2048, 2048], P('wt', 'ctx'), may hold values from -6 to 6
- segments: int32 [4, 2048], P('wt', 'ctx'), may hold values from 0 to 7, never falling along the last dimension, each value on 1 to 1024 neighbouring positions
- adapter_index: int32 [4], P('wt'), may hold values from 0 to 7
- first_gain: float32 [2048], replicated, may hold values from 0.1 to 1.9
- first_bias: float32 [2048], replicated, may hold values from -3 to 3
- second_gain: float32 [2048], replicated, may hold values from 0.1 to 1.9
- second_bias: float32 [2048], replicated, may hold values from -3 to 3
- qkv_weight: bfloat16 [2048, 2304], P('wt'), may hold values from -0.125 to 0.125
- out_weight: bfloat16 [2048, 2048], P('wt'), may hold values from -0.5 to 0.5
- expand_weight: bfloat16 [2048, 8192], P('wt'), may hold values from -0.125 to 0.125
- shrink_weight: bfloat16 [8192, 2048], P('wt'), may hold values from -0.0625 to 0.0625
- query_first: bfloat16 [8, 2048, 16], replicated, may hold values from -0.125 to 0.125
- query_second: bfloat16 [8, 16, 2048], replicated, may hold values from -1.5 to 1.5
- key_first: bfloat16 [8, 2048, 16], replicated, may hold values from -0.125 to 0.125
- key_second: bfloat16 [8, 16, 128], replicated, may hold values from -1.5 to 1.5
- value_first: bfloat16 [8, 2048, 16], replicated, may hold values from -0.125 to 0.125
- value_second: bfloat16 [8, 16, 128], replicated, may hold values from -1.5 to 1.5
- output_first: bfloat16 [8, 2048, 16], replicated, may hold values from -0.5 to 0.5
- output_second: bfloat16 [8, 16, 2048], replicated, may hold values from -1.5 to 1.5
- expand_first: bfloat16 [8, 2048, 16], replicated, may hold values from -0.125 to 0.125
- expand_second: bfloat16 [8, 16, 8192], replicated, may hold values from -1.5 to 1.5
- shrink_first: bfloat16 [8, 8192, 16], replicated, may hold values from -0.0625 to 0.0625
- shrink_second: bfloat16 [8, 16, 2048], replicated, may hold values from -1.5 to 1.5
Outputs:
- layer_out: bfloat16 [4, 2048, 2048], P('wt', 'ctx')
- tokens_grad: bfloat16 [4, 2048, 2048], P('wt', 'ctx')
- grad_query_first: float32 [8, 2048, 16], P(None, 'wt')
- grad_query_second: float32 [8, 16, 2048], P(None, None, 'wt')
- grad_key_first: float32 [8, 2048, 16], P(None, 'wt')
- grad_key_second: float32 [8, 16, 128], P(None, None, 'wt')
- grad_value_first: float32 [8, 2048, 16], P(None, 'wt')
- grad_value_second: float32 [8, 16, 128], P(None, None, 'wt')
- grad_output_first: float32 [8, 2048, 16], P(None, 'wt')
- grad_output_second: float32 [8, 16, 2048], P(None, None, 'wt')
- grad_expand_first: float32 [8, 2048, 16], P(None, 'wt')
- grad_expand_second: float32 [8, 16, 8192], P(None, None, 'wt')
- grad_shrink_first: float32 [8, 8192, 16], P(None, 'wt')
- grad_shrink_second: float32 [8, 16, 2048], P(None, None, 'wt')
Inputs may be any that keep to these rules, and one draw needn't show every extreme that they name: `segments`: within each sequence the numbers never fall; a document is a run of equal numbers of at most 1024 positions.
All inputs are finite; a program needn't handle non-finite values.
Results may differ from a plain program's by a relative error of at most 0.02.
Values may be sent and summed in bfloat16 or wider, within the bound.
A program may use at most 320 MiB of HBM per device.

v0:
```python
import math
import jax
import jax.numpy as jnp
from jax import lax
from jax.sharding import PartitionSpec as P

HEADS = 16
HEAD = 128
ADAPTERS = 8
KEY_BLOCK = 512
EPSILON = 1e-05
LOWEST = -1e30


def matmul(left, right):
    return jnp.dot(left, right, preferred_element_type=jnp.float32)


def matmul_right_t(left, right):
    return lax.dot_general(
        left, right, (((1,), (1,)), ((), ())), preferred_element_type=jnp.float32
    )


def matmul_left_t(left, right):
    return lax.dot_general(
        left, right, (((0,), (0,)), ((), ())), preferred_element_type=jnp.float32
    )


def layer_norm(values, gain, offset):
    centre = values - jnp.mean(values, -1, keepdims=True)
    scale_inv = lax.rsqrt(jnp.mean(centre * centre, -1, keepdims=True) + EPSILON)
    normed = centre * scale_inv
    return (normed * gain + offset, normed, scale_inv)


def norm_back(grad_out, gain, normed, scale_inv):
    grad_norm = grad_out * gain
    return scale_inv * (
        grad_norm
        - jnp.mean(grad_norm, -1, keepdims=True)
        - normed * jnp.mean(grad_norm * normed, -1, keepdims=True)
    )


def gelu_tanh(values):
    return jax.nn.gelu(values, approximate=True)


def fold_rows(left, piece):
    return matmul(left, piece)


def project_back(grad_low, piece):
    return matmul_right_t(grad_low, piece)


def spread_table(onehot, table):
    return onehot[:, None, None] * table[None]


def body(
    tokens,
    out_grad,
    segments,
    adapter_index,
    first_gain,
    first_bias,
    second_gain,
    second_bias,
    qkv_weight,
    out_weight,
    expand_weight,
    shrink_weight,
    query_first,
    query_second,
    key_first,
    key_second,
    value_first,
    value_second,
    output_first,
    output_second,
    expand_first,
    expand_second,
    shrink_first,
    shrink_second,
):
    hidden = tokens[0].astype(jnp.float32)
    tok_count = hidden.shape[0]
    model_width = hidden.shape[1]
    chosen = adapter_index[0]

    def select(table):
        return lax.dynamic_index_in_dim(table, chosen, 0, keepdims=False)

    own_query_first = select(query_first)
    own_query_second = select(query_second)
    own_key_first = select(key_first)
    own_key_second = select(key_second)
    own_value_first = select(value_first)
    own_value_second = select(value_second)
    own_output_first = select(output_first)
    own_output_second = select(output_second)
    own_expand_first = select(expand_first)
    own_expand_second = select(expand_second)
    own_shrink_first = select(shrink_first)
    own_shrink_second = select(shrink_second)
    rank_width = own_query_first.shape[1]
    score_scale = 1.0 / math.sqrt(HEAD)
    normed_one, plain_one, inverse_one = layer_norm(hidden, first_gain, first_bias)
    first_low = normed_one.astype(jnp.bfloat16)
    attn_first = jnp.concatenate([own_query_first, own_key_first, own_value_first], 1)
    low_rank = matmul(first_low, attn_first).astype(jnp.bfloat16)
    base = fold_rows(first_low, lax.all_gather(qkv_weight, "wt", axis=0, tiled=True))
    query = (
        (base[:, :model_width] + matmul(low_rank[:, :rank_width], own_query_second))
        .astype(jnp.bfloat16)
        .reshape(tok_count, HEADS, HEAD)
    )
    keys_own = (
        base[:, model_width : model_width + HEAD]
        + matmul(low_rank[:, rank_width : 2 * rank_width], own_key_second)
    ).astype(jnp.bfloat16)
    values_own = (
        base[:, model_width + HEAD :] + matmul(low_rank[:, 2 * rank_width :], own_value_second)
    ).astype(jnp.bfloat16)
    keys_all, values_all, segs_all = (
        lax.all_gather(keys_own, "ctx", axis=0, tiled=True),
        lax.all_gather(values_own, "ctx", axis=0, tiled=True),
        lax.all_gather(segments[0], "ctx", axis=0, tiled=True),
    )
    query_segs = segments[0]
    position = lax.axis_index("ctx") * tok_count + jnp.arange(tok_count, dtype=jnp.int32)
    first_block = jnp.sum((segs_all < query_segs[0]).astype(jnp.int32)) // KEY_BLOCK
    stop_block = position[tok_count - 1] // KEY_BLOCK + 1
    offsets = jnp.arange(KEY_BLOCK, dtype=jnp.int32)

    def block_scores(start):
        key_block = lax.dynamic_slice_in_dim(keys_all, start, KEY_BLOCK, 0)
        value_block = lax.dynamic_slice_in_dim(values_all, start, KEY_BLOCK, 0)
        seg_block = lax.dynamic_slice_in_dim(segs_all, start, KEY_BLOCK, 0)
        allowed = (query_segs[:, None] == seg_block[None, :]) & (
            position[:, None] >= start + offsets[None, :]
        )
        raw = (
            jnp.einsum("thd,kd->thk", query, key_block, preferred_element_type=jnp.float32)
            * score_scale
        )
        return (jnp.where(allowed[:, None, :], raw, LOWEST), allowed, key_block, value_block)

    def stats_step(index, carry):
        highest, total = carry
        scores, allowed, key_block, value_block = block_scores(index * KEY_BLOCK)
        new_high = jnp.maximum(highest, jnp.max(scores, -1))
        weights = jnp.where(allowed[:, None, :], jnp.exp(scores - new_high[..., None]), 0.0)
        return (new_high, total * jnp.exp(highest - new_high) + jnp.sum(weights, -1))

    highest, total = lax.fori_loop(
        first_block,
        stop_block,
        stats_step,
        (
            jnp.full((tok_count, HEADS), LOWEST, jnp.float32),
            jnp.zeros((tok_count, HEADS), jnp.float32),
        ),
    )
    log_total = highest + jnp.log(total)

    def value_step(index, gathered):
        scores, allowed, key_block, value_block = block_scores(index * KEY_BLOCK)
        probs = jnp.where(allowed[:, None, :], jnp.exp(scores - log_total[..., None]), 0.0).astype(
            jnp.bfloat16
        )
        return gathered + jnp.einsum(
            "thk,kd->thd", probs, value_block, preferred_element_type=jnp.float32
        )

    attended = lax.fori_loop(
        first_block, stop_block, value_step, jnp.zeros((tok_count, HEADS, HEAD), jnp.float32)
    )
    attended_low = attended.reshape(tok_count, model_width).astype(jnp.bfloat16)
    output_low = matmul(attended_low, own_output_first).astype(jnp.bfloat16)
    branch = fold_rows(attended_low, lax.all_gather(out_weight, "wt", axis=0, tiled=True))
    middle = hidden + branch + matmul(output_low, own_output_second)
    normed_two, plain_two, inverse_two = layer_norm(middle, second_gain, second_bias)
    second_low = normed_two.astype(jnp.bfloat16)
    expand_low = matmul(second_low, own_expand_first).astype(jnp.bfloat16)
    upward = fold_rows(
        second_low, lax.all_gather(expand_weight, "wt", axis=0, tiled=True)
    ) + matmul(expand_low, own_expand_second)
    active, gelu_pull = jax.vjp(gelu_tanh, upward)
    active_low = active.astype(jnp.bfloat16)
    shrink_low = matmul(active_low, own_shrink_first).astype(jnp.bfloat16)
    shrunk = fold_rows(active_low, lax.all_gather(shrink_weight, "wt", axis=0, tiled=True))
    layer_out = (middle + shrunk + matmul(shrink_low, own_shrink_second)).astype(jnp.bfloat16)[None]
    grad_low = out_grad[0]
    grad_top = grad_low.astype(jnp.float32)
    grad_shrink_low = matmul_right_t(grad_low, own_shrink_second).astype(jnp.bfloat16)
    grad_active = project_back(
        grad_low, lax.all_gather(shrink_weight, "wt", axis=0, tiled=True)
    ) + matmul_right_t(grad_shrink_low, own_shrink_first)
    shrink_second_grad = matmul_left_t(shrink_low, grad_low)
    shrink_first_grad = matmul_left_t(active_low, grad_shrink_low)
    grad_active_low = grad_active.astype(jnp.bfloat16)
    grad_upward = gelu_pull(grad_active_low.astype(jnp.float32))[0].astype(jnp.bfloat16)
    grad_expand_low = matmul_right_t(grad_upward, own_expand_second).astype(jnp.bfloat16)
    grad_second = project_back(
        grad_upward, lax.all_gather(expand_weight, "wt", axis=0, tiled=True)
    ) + matmul_right_t(grad_expand_low, own_expand_first)
    expand_second_grad = matmul_left_t(expand_low, grad_upward)
    expand_first_grad = matmul_left_t(second_low, grad_expand_low)
    grad_middle = grad_top + norm_back(grad_second, second_gain, plain_two, inverse_two)
    grad_branch = grad_middle.astype(jnp.bfloat16)
    grad_output_low = matmul_right_t(grad_branch, own_output_second).astype(jnp.bfloat16)
    grad_attended = project_back(
        grad_branch, lax.all_gather(out_weight, "wt", axis=0, tiled=True)
    ) + matmul_right_t(grad_output_low, own_output_first)
    output_second_grad = matmul_left_t(output_low, grad_branch)
    output_first_grad = matmul_left_t(attended_low, grad_output_low)
    grad_attn_low = grad_attended.astype(jnp.bfloat16).reshape(tok_count, HEADS, HEAD)
    delta = jnp.sum(grad_attn_low.astype(jnp.float32) * attended, -1)
    seq_length = keys_all.shape[0]

    def back_step(index, carry):
        grad_query, grad_keys, grad_values = carry
        start = index * KEY_BLOCK
        scores, allowed, key_block, value_block = block_scores(start)
        probs = jnp.where(allowed[:, None, :], jnp.exp(scores - log_total[..., None]), 0.0)
        probs_low = probs.astype(jnp.bfloat16)
        grad_probs = jnp.einsum(
            "thd,kd->thk", grad_attn_low, value_block, preferred_element_type=jnp.float32
        )
        grad_scores = (probs * (grad_probs - delta[..., None])).astype(jnp.bfloat16)
        grad_query = grad_query + jnp.einsum(
            "thk,kd->thd", grad_scores, key_block, preferred_element_type=jnp.float32
        )
        key_part = jnp.einsum("thk,thd->kd", grad_scores, query, preferred_element_type=jnp.float32)
        value_part = jnp.einsum(
            "thk,thd->kd", probs_low, grad_attn_low, preferred_element_type=jnp.float32
        )
        grad_keys = lax.dynamic_update_slice_in_dim(grad_keys, key_part, start, 0)
        grad_values = lax.dynamic_update_slice_in_dim(grad_values, value_part, start, 0)
        return (grad_query, grad_keys, grad_values)

    start_carry = (
        jnp.zeros((tok_count, HEADS, HEAD), jnp.float32),
        jnp.zeros((seq_length, HEAD), jnp.float32),
        jnp.zeros((seq_length, HEAD), jnp.float32),
    )
    grad_query, grad_keys, grad_values = lax.fori_loop(
        first_block, stop_block, back_step, start_carry
    )
    own_key_grad, own_value_grad = (
        lax.psum_scatter(
            (grad_keys * score_scale).astype(jnp.bfloat16), "ctx", scatter_dimension=0, tiled=True
        ).astype(jnp.float32),
        lax.psum_scatter(
            grad_values.astype(jnp.bfloat16), "ctx", scatter_dimension=0, tiled=True
        ).astype(jnp.float32),
    )
    grad_query_low = (grad_query * score_scale).reshape(tok_count, model_width).astype(jnp.bfloat16)
    own_key_low = own_key_grad.astype(jnp.bfloat16)
    own_value_low = own_value_grad.astype(jnp.bfloat16)
    grad_qkv_low = jnp.concatenate([grad_query_low, own_key_low, own_value_low], 1)
    grad_rank = jnp.concatenate(
        [
            matmul_right_t(grad_query_low, own_query_second),
            matmul_right_t(own_key_low, own_key_second),
            matmul_right_t(own_value_low, own_value_second),
        ],
        1,
    ).astype(jnp.bfloat16)
    grad_first = project_back(
        grad_qkv_low, lax.all_gather(qkv_weight, "wt", axis=0, tiled=True)
    ) + matmul_right_t(grad_rank, attn_first)
    query_second_grad = matmul_left_t(low_rank[:, :rank_width], grad_query_low)
    key_second_grad = matmul_left_t(low_rank[:, rank_width : 2 * rank_width], own_key_low)
    value_second_grad = matmul_left_t(low_rank[:, 2 * rank_width :], own_value_low)
    attn_first_grad = matmul_left_t(first_low, grad_rank)
    query_first_grad = attn_first_grad[:, :rank_width]
    key_first_grad = attn_first_grad[:, rank_width : 2 * rank_width]
    value_first_grad = attn_first_grad[:, 2 * rank_width :]
    tokens_grad = (grad_middle + norm_back(grad_first, first_gain, plain_one, inverse_one)).astype(
        jnp.bfloat16
    )[None]
    onehot = (jnp.arange(ADAPTERS, dtype=jnp.int32) == chosen).astype(jnp.float32)
    summed = lax.psum(
        (
            spread_table(onehot, query_first_grad),
            spread_table(onehot, query_second_grad),
            spread_table(onehot, key_first_grad),
            spread_table(onehot, key_second_grad),
            spread_table(onehot, value_first_grad),
            spread_table(onehot, value_second_grad),
            spread_table(onehot, output_first_grad),
            spread_table(onehot, output_second_grad),
            spread_table(onehot, expand_first_grad),
            spread_table(onehot, expand_second_grad),
            spread_table(onehot, shrink_first_grad),
            spread_table(onehot, shrink_second_grad),
        ),
        ("ctx", "wt"),
    )
    member = lax.axis_index("wt")
    members = lax.axis_size("wt")
    shares = []
    for number, table in enumerate(summed):
        axis_dim = 1 + number % 2
        share_len = table.shape[axis_dim] // members
        shares.append(lax.dynamic_slice_in_dim(table, member * share_len, share_len, axis_dim))
    return (
        layer_out,
        tokens_grad,
        shares[0],
        shares[1],
        shares[2],
        shares[3],
        shares[4],
        shares[5],
        shares[6],
        shares[7],
        shares[8],
        shares[9],
        shares[10],
        shares[11],
    )


def solution(mesh):
    placed = (
        P("wt", "ctx", None),
        P("wt", "ctx", None),
        P("wt", "ctx"),
        P("wt"),
        P(),
        P(),
        P(),
        P(),
        P("wt", None),
        P("wt", None),
        P("wt", None),
        P("wt", None),
        P(),
        P(),
        P(),
        P(),
        P(),
        P(),
        P(),
        P(),
        P(),
        P(),
        P(),
        P(),
    )
    return jax.shard_map(
        body,
        mesh=mesh,
        in_specs=placed,
        out_specs=(
            P("wt", "ctx", None),
            P("wt", "ctx", None),
            P(None, "wt", None),
            P(None, None, "wt"),
            P(None, "wt", None),
            P(None, None, "wt"),
            P(None, "wt", None),
            P(None, None, "wt"),
            P(None, "wt", None),
            P(None, None, "wt"),
            P(None, "wt", None),
            P(None, None, "wt"),
            P(None, "wt", None),
            P(None, None, "wt"),
        ),
        check_vma=False,
    )
```

profile of v0, /device:TPU:0, one launch (start us, length us, event | category | flops | bytes accessed | tf_op | source)
XLA Modules:
  0.0 1124.4 jit_solution(9140331551840397132)
XLA Ops:
  10.6 22.3 %all-gather = s32[1,2048]{1,0:T(1,128)S(1)} all-gather(s32[1,256]{1,0:T(1,128)S(1)} %copy-done.26), channel_id=2, replica_groups=mesh['ctx'=8,'wt'=4] {'ctx'}, dimensions={1}, use_global_device_ids=true | all-gather | bytes 9216 | tf_op jit(solution)/shard_map/all_gather | solution.py:131
  48.1 28.4 %all-gather.6.cloned.1.call-done = bf16[2048,2304]{1,0:T(8,128)(2,1)} async-done(((bf16[512,2304]{1,0:T(8,128)(2,1)}), bf16[2048,2304]{1,0:T(8,128)(2,1)}) %all-gather.6.cloned.1.call-update) | async-done | bytes 9437200 | tf_op jit(solution)/shard_map/all_gather | solution.py:115
  76.5 6.6 fusion.188
  86.7 33.2 %all_gather.27 = bf16[2048,128]{1,0:T(8,128)(2,1)} all-gather(bf16[256,128]{1,0:T(8,128)(2,1)S(1)} %fusion.109), channel_id=1, replica_groups=mesh['ctx'=8,'wt'=4] {'ctx'}, dimensions={0}, use_global_device_ids=true | all-gather | bytes 589824 | tf_op jit(solution)/shard_map/all_gather | solution.py:129
  120.3 4.7 while.39
  126.1 37.9 %all_gather.28 = bf16[2048,128]{1,0:T(8,128)(2,1)} all-gather(bf16[256,128]{1,0:T(8,128)(2,1)S(1)} %fusion.110), channel_id=1, replica_groups=mesh['ctx'=8,'wt'=4] {'ctx'}, dimensions={0}, use_global_device_ids=true | all-gather | bytes 589824 | tf_op jit(solution)/shard_map/all_gather | solution.py:130
  165.6 6.6 while.40
  165.8 6.1 fusion.271
  172.1 2.5 copy.45
  176.2 6.3 fusion.83
  188.0 151.6 %all-gather.10.cloned.1.call-done = bf16[2048,8192]{1,0:T(8,128)(2,1)} async-done(((bf16[512,8192]{1,0:T(8,128)(2,1)}), bf16[2048,8192]{1,0:T(8,128)(2,1)}) %all-gather.10.cloned.1.call-update) | async-done | bytes 33554448 | tf_op jit(solution)/shard_map/all_gather | solution.py:190
  339.6 22.7 %fusion.189 = f32[256,8192]{1,0:T(8,128)} fusion(bf16[256,2048]{1,0:T(8,128)(2,1)} %copy-done.17, bf16[2048,8192]{1,0:T(8,128)(2,1)} %all-gather.10.cloned.1.call-done), kind=kOutput, calls=%fused_computation.265 | convolution fusion | flops 8589934592 | bytes 42991616 | tf_op jit(solution)/shard_map/dot_general | solution.py:16
  362.2 10.3 multiply_convert_fusion
  372.6 169.9 %all-gather.12.cloned.1.call-done = bf16[8192,2048]{1,0:T(8,128)(2,1)} async-done(((bf16[2048,2048]{1,0:T(8,128)(2,1)}), bf16[8192,2048]{1,0:T(8,128)(2,1)}) %all-gather.12.cloned.1.call-update) | async-done | bytes 33554448 | tf_op jit(solution)/shard_map/all_gather | solution.py:195
  542.5 18.5 %fusion.115 = f32[256,8192]{1,0:T(8,128)} fusion(bf16[8192,2048]{1,0:T(8,128)(2,1)} %all-gather.12.cloned.1.call-done, bf16[1,256,2048]{2,1,0:T(8,128)(2,1)} %param.31), kind=kOutput, calls=%fused_computation.152 | convolution fusion | flops 8589934592 | bytes 42991616 | tf_op jit(solution)/shard_map/dot_general | solution.py:20
  561.0 24.8 %fusion.73 = bf16[256,8192]{1,0:T(8,128)(2,1)S(1)} fusion(f32[256,8192]{1,0:T(8,128)} %get-tuple-element.439, f32[256,8192]{1,0:T(8,128)} %fusion.115, bf16[16,256]{1,0:T(8,128)(2,1)S(1)} %convolution_convert_fusion.6, bf16[8,8192,16]{1,2,0:T(8,128)(2,1)} %param.52, s32[]{:T(128)S(6)} %select_n.82), kind=kOutput, calls=%fused_computation.77 | convolution fusion | flops 115343360 | bytes 21241860 | tf_op jit(solution)/shard_map/dot_general | solution.py:20
  589.1 17.0 %fusion.190 = f32[256,2048]{1,0:T(8,128)} fusion(bf16[256,8192]{1,0:T(8,128)(2,1)} %copy-done.13, bf16[2048,8192]{1,0:T(8,128)(2,1)} %all-gather.10.cloned.1.call-done), kind=kOutput, calls=%fused_computation.266 | convolution fusion | flops 8589934592 | bytes 39845888 | tf_op jit(solution)/shard_map/dot_general | solution.py:20
  606.1 2.6 fusion.185
  611.9 2.4 fusion.182
  625.0 15.0 %while.41 = (s32[]{:T(128)}, f32[256,16,128]{2,0,1:T(8,128)S(1)}, f32[2048,128]{0,1:T(8,128)}, bf16[2048,128]{0,1:T(8,128)(2,1)}, s32[]{:T(128)}, /*index=5*/s32...) while((s32[]{:T(128)}, f32[256,16,128]{2,0,1:T(8,128)S(1)}, ...), condition=%wide.region_15.16_spmd.clone, body=%wide.region_14.15_spmd.clone.sunk | while | flops 2710438656 | bytes 55899472 | solution.py:251
  627.6 4.1 fusion.283
  631.7 2.6 convolution_add_fusion.13
  636.5 2.5 fusion.285
  640.1 3.8 broadcast_multiply_fusion.1
  643.9 2.5 broadcast_multiply_fusion
  655.2 2.8 broadcast_multiply_fusion.2
  658.0 74.1 %reduce-scatter.5.cloned.1.call-done = bf16[256,128]{0,1:T(8,128)(2,1)} async-done(((bf16[2048,128]{0,1:T(8,128)(2,1)}), bf16[256,128]{0,1:T(8,128)(2,1)}) %reduce-scatter.5.cloned.1.call-update) | async-done | bytes 65552 | tf_op jit(solution)/shard_map/reduce_scatter | solution.py:258
  733.1 65.0 %reduce-scatter.3.cloned.1.call-done = bf16[256,128]{0,1:T(8,128)(2,1)} async-done(((bf16[2048,128]{0,1:T(8,128)(2,1)}), bf16[256,128]{0,1:T(8,128)(2,1)}) %reduce-scatter.3.cloned.1.call-update) | async-done | bytes 65552 | tf_op jit(solution)/shard_map/reduce_scatter | solution.py:255
  803.4 2.5 broadcast_multiply_fusion.3
  807.6 17.9 %convolution_add_fusion.9 = f32[256,2048]{1,0:T(8,128)S(1)} fusion(f32[256,2048]{1,0:T(8,128)S(1)} %copy-done.4, bf16[256,8192]{1,0:T(8,128)(2,1)} %get-tuple-element.438, bf16[8192,2048]{1,0:T(8,128)(2,1)} %all-gather.12.cloned.1.call-done), kind=kOutput, calls=%fused_computation.98 | convolution fusion | flops 8590458880 | bytes 41943040 | tf_op jit(solution)/shard_map/dot_general | solution.py:16
  827.8 5.6 fusion.103
  836.9 259.0 %all-reduce.3.cloned.1.call-done = (f32[8,2048,16]{1,2,0:T(8,128)}, f32[8,16,2048]{2,1,0:T(8,128)}, f32[8,2048,16]{1,2,0:T(8,128)}, f32[8,16,128]{2,1,0:T(8,128)...) async-done(((f32[8,2048,16]{1,2,0:T(8,128)}, ...) | async-done | bytes 16908304 | tf_op jit(solution)/shard_map/psum | solution.py:288
  (218 shorter events, 96.9 us)
Async XLA Ops:
  7.2 355.1 %copy-start = (bf16[8,16,8192]{2,1,0:T(8,128)(2,1)S(1)}, bf16[8,16,8192]{2,1,0:T(8,128)(2,1)}, u32[]{:S(2)}) copy-start(bf16[8,16,8192]{2,1,0:T(8,128)(2,1)} %param.51) | copy-start | bytes 6291460
  7.2 69.3 %all-gather.6.cloned.1.call-start = ((), (), s32[]{:S(2)}) async-start(), calls=%async_computation.2 | async-start | bytes 11796480 | tf_op jit(solution)/shard_map/all_gather | solution.py:115
  7.9 168.3 %all-gather.8.cloned.1.call-start = ((), (), s32[]{:S(2)}) async-start(), calls=%async_computation.3 | async-start | bytes 10485760 | tf_op jit(solution)/shard_map/all_gather | solution.py:184
  8.7 330.9 %all-gather.10.cloned.1.call-start = ((), (), s32[]{:S(2)}) async-start(), calls=%async_computation.4 | async-start | bytes 41943040 | tf_op jit(solution)/shard_map/all_gather | solution.py:190
  9.4 31.8 %copy-start.5 = (bf16[1,256,2048]{2,1,0:T(8,128)(2,1)S(1)}, bf16[1,256,2048]{2,1,0:T(8,128)(2,1)}, u32[]{:S(2)}) copy-start(bf16[1,256,2048]{2,1,0:T(8,128)(2,1)} %param.30) | copy-start | bytes 3145732
  9.4 533.1 %all-gather.12.cloned.1.call-start = ((), (), s32[]{:S(2)}) async-start(), calls=%async_computation.5 | async-start | bytes 41943040 | tf_op jit(solution)/shard_map/all_gather | solution.py:195
  10.0 36.2 %copy-start.41 = (f32[2048]{0:T(1024)S(1)}, f32[2048]{0:T(1024)}, u32[]{:S(2)}) copy-start(f32[2048]{0:T(1024)} %param.34) | copy-start | bytes 24580
  10.0 36.2 %copy-start.49 = (f32[2048]{0:T(1024)S(1)}, f32[2048]{0:T(1024)}, u32[]{:S(2)}) copy-start(f32[2048]{0:T(1024)} %param.35) | copy-start | bytes 24580
  10.0 722.1 %reduce-scatter.5.cloned.1.call-start = ((), (), s32[]{:S(2)}) async-start(), calls=%async_computation.7 | async-start | bytes 589824 | tf_op jit(solution)/shard_map/reduce_scatter | solution.py:258
  42.8 40.4 %copy-start.27 = (bf16[2048,16]{0,1:T(8,128)(2,1)}, bf16[2048,16]{0,1:T(8,128)(2,1)S(1)}, u32[]{:S(2)}) copy-start(bf16[2048,16]{0,1:T(8,128)(2,1)S(1)} %dynamic-slice_bitcast_fusion.2) | copy-start | bytes 196612
  43.7 39.5 %copy-start.29 = (bf16[2048,16]{0,1:T(8,128)(2,1)}, bf16[2048,16]{0,1:T(8,128)(2,1)S(1)}, u32[]{:S(2)}) copy-start(bf16[2048,16]{0,1:T(8,128)(2,1)S(1)} %get-tuple-element.442) | copy-start | bytes 196612
  43.7 39.5 %copy-start.31 = (bf16[2048,16]{0,1:T(8,128)(2,1)}, bf16[2048,16]{0,1:T(8,128)(2,1)S(1)}, u32[]{:S(2)}) copy-start(bf16[2048,16]{0,1:T(8,128)(2,1)S(1)} %get-tuple-element.443) | copy-start | bytes 196612
  48.1 76.9 %copy-start.35 = (bf16[256,48]{0,1:T(8,128)(2,1)}, bf16[256,48]{0,1:T(8,128)(2,1)S(1)}, u32[]{:S(2)}) copy-start(bf16[256,48]{0,1:T(8,128)(2,1)S(1)} %convolution_convert_fusion) | copy-start | bytes 73732
  83.2 37.0 %copy-start.21 = (f32[256,2304]{1,0:T(8,128)}, f32[256,2304]{1,0:T(8,128)S(1)}, u32[]{:S(2)}) copy-start(f32[256,2304]{1,0:T(8,128)S(1)} %fusion.188) | copy-start | bytes 7077892
  176.2 6.3 copy-start.37
  589.1 17.0 %copy-start.3 = (f32[256,2048]{1,0:T(8,128)S(1)}, f32[256,2048]{1,0:T(8,128)}, u32[]{:S(2)}) copy-start(f32[256,2048]{1,0:T(8,128)} %copy-done.2) | copy-start | bytes 6291460
  625.0 15.1 %copy-start.47 = (f32[8]{0:T(128)S(1)}, f32[8]{0:T(128)}, u32[]{:S(2)}) copy-start(f32[8]{0:T(128)} %compare_convert_fusion) | copy-start | bytes 100
  640.0 6.3 copy-start.16
  640.1 158.1 %reduce-scatter.3.cloned.1.call-start = ((), (), s32[]{:S(2)}) async-start(), calls=%async_computation.6 | async-start | bytes 589824 | tf_op jit(solution)/shard_map/reduce_scatter | solution.py:255
  648.5 6.4 copy-start.8
  648.5 6.4 copy-start.38
  653.2 442.8 %all-reduce.3.cloned.1.call-start = ((), (), s32[]{:S(2)}) async-start(), calls=%async_computation.8 | async-start | bytes 33816576 | tf_op jit(solution)/shard_map/psum | solution.py:288
  655.2 145.5 %copy-start.36 = (bf16[256,48]{0,1:T(8,128)(2,1)S(1)}, bf16[256,48]{0,1:T(8,128)(2,1)}, u32[]{:S(2)}) copy-start(bf16[256,48]{0,1:T(8,128)(2,1)} %copy-done.35) | copy-start | bytes 73732
  655.2 147.5 %copy-start.48 = (f32[8]{0:T(128)S(1)}, f32[8]{0:T(128)}, u32[]{:S(2)}) copy-start(f32[8]{0:T(128)} %compare_convert_fusion) | copy-start | bytes 100
  807.6 20.2 %copy-start.33 = (bf16[256,128]{0,1:T(8,128)(2,1)S(1)}, bf16[256,128]{0,1:T(8,128)(2,1)}, u32[]{:S(2)}) copy-start(bf16[256,128]{0,1:T(8,128)(2,1)} %reduce-scatter.5.cloned.1.call-done) | copy-start | bytes 196612
  807.6 20.2 %copy-start.34 = (bf16[256,128]{0,1:T(8,128)(2,1)S(1)}, bf16[256,128]{0,1:T(8,128)(2,1)}, u32[]{:S(2)}) copy-start(bf16[256,128]{0,1:T(8,128)(2,1)} %reduce-scatter.3.cloned.1.call-done) | copy-start | bytes 196612
  827.8 5.7 copy-start.28
  827.8 5.8 copy-start.30
  827.8 5.7 copy-start.32
  827.8 5.7 copy-start.39
  827.8 5.7 copy-start.42
  1096.0 21.2 %copy-start.1 = (bf16[8,16,8192]{2,1,0:T(8,128)(2,1)S(1)}, bf16[8,16,8192]{2,1,0:T(8,128)(2,1)}, u32[]{:S(2)}) copy-start(bf16[8,16,8192]{2,1,0:T(8,128)(2,1)} %param.51) | copy-start | bytes 6291460
  (28 other events, 86.3 us)
Sparse Core Ops, SparseCore 0:
  9.6 66.9 all-gather.5
  78.1 58.2 all-gather.7
  138.0 201.5 all-gather.9
  341.0 201.4 all-gather.11
  640.2 91.9 reduce-scatter.4
  735.9 62.1 reduce-scatter.2
  806.1 289.8 all-reduce.2
where the time goes:
time: 1130 us; the launch traced here: 1120 us
  waiting for transfers between devices  751 us (66%)
  matrix products  190 us (17%)
  blocking collectives  93.4 us (8%)
  local copies, waits for them, and re-layouts  42.9 us (4%)
  other arithmetic  25.7 us (2%)
  between operations  21.2 us (2%)
    psum x1, waiting for transfers between devices, body(): lax.psum((spread_table(onehot, query_first_grad), spread_table(onehot, qu...  259 us
    all_gather x1, waiting for transfers between devices, body(): lax.all_gather(shrink_weight, 'wt', axis=0, tiled=True)  170 us
    all_gather x1, waiting for transfers between devices, body(): lax.all_gather(expand_weight, 'wt', axis=0, tiled=True)  152 us
    dot_general x14, matrix products, matmul_right_t(): lax.dot_general(left, right, (((1,), (1,)), ((), ())), preferred_element_...  82.1 us
    dot_general x14, matrix products, matmul(): return jnp.dot(left, right, preferred_element_type=jnp.float32)  76.2 us
    reduce_scatter x1, waiting for transfers between devices, body(): lax.psum_scatter(grad_values.astype(jnp.bfloat16), 'ctx', scatter_dimensi...  74.1 us
    reduce_scatter x1, waiting for transfers between devices, body(): lax.psum_scatter((grad_keys * score_scale).astype(jnp.bfloat16), 'ctx', s...  65 us
    all_gather x1, blocking collectives, body(): lax.all_gather(values_own, 'ctx', axis=0, tiled=True)  37.9 us
  transfers between devices with their start and end apart: 7, of which 6 were waited for; matrix products, arithmetic and copies ran while one was open for 11% of the time, Pallas kernels for 0%

commit v1 on v0

--- a/solution.py
+++ b/solution.py
@@ -1,3 +1,4 @@
+import functools
 import math
 import jax
 import jax.numpy as jnp
@@ -10,6 +11,42 @@
 KEY_BLOCK = 512
 EPSILON = 1e-05
 LOWEST = -1e30
+
+
+def convert_the_pipes(frame, ndim_at):
+    frame = jnp.moveaxis(frame, 0, ndim_at)
+    item_now = frame.shape
+    state_now = frame.reshape(
+        *item_now[:ndim_at], item_now[ndim_at] * item_now[ndim_at + 1], *item_now[ndim_at + 2 :]
+    )
+    return state_now
+
+
+def lift_links_up(block_in, row_axis):
+    n_dev_all = lax.psum(1, axis_name=row_axis)
+    r2 = block_in[None]
+    for kk in range(n_dev_all.bit_length() - 1):
+        small = 1 << kk
+        ledger = []
+        i = 0
+        while i < n_dev_all:
+            ledger.append((i, i ^ small))
+            i = i + 1
+        z_new = lax.ppermute(r2, axis_name=row_axis, perm=ledger)
+        found_now = jnp.stack([r2, z_new], 0)
+        mat_out = lax.axis_index(row_axis)
+        long_array = mat_out >> kk & 1
+        r2 = jnp.where(long_array == 0, found_now, found_now[::-1]).reshape(-1, *block_in.shape)
+    return r2
+
+
+def read_the_tables(own_rows, x_in, which_dim):
+    x_now = lift_links_up(own_rows, x_in)
+    opened = convert_the_pipes(x_now, which_dim)
+    return opened
+
+
+reach_the_levels_all = functools.partial(read_the_tables, x_in="wt", which_dim=0)
 
 
 def matmul(left, right):
@@ -112,7 +149,7 @@
     first_low = normed_one.astype(jnp.bfloat16)
     attn_first = jnp.concatenate([own_query_first, own_key_first, own_value_first], 1)
     low_rank = matmul(first_low, attn_first).astype(jnp.bfloat16)
-    base = fold_rows(first_low, lax.all_gather(qkv_weight, "wt", axis=0, tiled=True))
+    base = fold_rows(first_low, reach_the_levels_all(qkv_weight))
     query = (
         (base[:, :model_width] + matmul(low_rank[:, :rank_width], own_query_second))
         .astype(jnp.bfloat16)

time: 1130 us -> 1200 us (1.062)
  waiting for transfers between devices: 751 us -> 796 us
  other arithmetic: 25.7 us -> 52.8 us
    ppermute x0 -> x2, waiting for transfers between devices: none -> 151 us  [lift_links_up(): z_new = lax.ppermute(r2, axis_name=row_axis, perm=ledger)]
    all_gather x1, waiting for transfers between devices: 152 us -> 12.4 us  [body(): lax.all_gather(expand_weight, 'wt', axis=0, tiled=True)]
    psum x1, waiting for transfers between devices: 259 us -> 289 us  [body(): lax.psum((spread_table(onehot, query_first_grad), spread_table(onehot, qu...]
    another operation x0 -> x3, other arithmetic: none -> 16.5 us  [lift_links_up(): found_now = jnp.stack([r2, z_new], 0)]
    select_n x0 -> x1, other arithmetic: none -> 12.3 us  [lift_links_up(): jnp.where(long_array == 0, found_now, found_now[::-1])]
  transfers between devices with their start and end apart: 7 -> 9, of which waited for: 6 -> 8; matrix products, arithmetic and copies ran while one was open for 11% -> 14% of each run, Pallas kernels for 0% -> 0%
where the time goes in v1:
time: 1200 us; the launch traced here: 1190 us
  waiting for transfers between devices  796 us (66%)
  matrix products  184 us (15%)
  blocking collectives  92.3 us (8%)
  other arithmetic  52.8 us (4%)
  local copies, waits for them, and re-layouts  42.7 us (4%)
  between operations  21.1 us (2%)
    psum x1, waiting for transfers between devices, body(): lax.psum((spread_table(onehot, query_first_grad), spread_table(onehot, qu...  289 us
    all_gather x1, waiting for transfers between devices, body(): lax.all_gather(shrink_weight, 'wt', axis=0, tiled=True)  170 us
    ppermute x2, waiting for transfers between devices, lift_links_up(): z_new = lax.ppermute(r2, axis_name=row_axis, perm=ledger)  151 us
    dot_general x14, matrix products, matmul_right_t(): lax.dot_general(left, right, (((1,), (1,)), ((), ())), preferred_element_...  79.5 us
    dot_general x14, matrix products, matmul(): return jnp.dot(left, right, preferred_element_type=jnp.float32)  76.7 us
    reduce_scatter x1, waiting for transfers between devices, body(): lax.psum_scatter(grad_values.astype(jnp.bfloat16), 'ctx', scatter_dimensi...  70.9 us
    reduce_scatter x1, waiting for transfers between devices, body(): lax.psum_scatter((grad_keys * score_scale).astype(jnp.bfloat16), 'ctx', s...  65 us
    all_gather x1, blocking collectives, body(): lax.all_gather(values_own, 'ctx', axis=0, tiled=True)  37.9 us
  transfers between devices with their start and end apart: 9, of which 8 were waited for; matrix products, arithmetic and copies ran while one was open for 14% of the time, Pallas kernels for 0%

profile of v1, /device:TPU:0, one launch (start us, length us, event | category | flops | bytes accessed | tf_op | source)
XLA Modules:
  0.0 1194.5 jit_solution(16879716331603967330)
XLA Ops:
  10.0 4.5 collective-permute-done
  14.5 2.8 pad_maximum_fusion.1
  17.4 5.4 fusion.82
  22.8 3.2 collective-permute-start.1
  26.5 21.0 %all-gather = s32[1,2048]{1,0:T(1,128)S(1)} all-gather(s32[1,256]{1,0:T(1,128)S(1)} %copy-done.26), channel_id=2, replica_groups=mesh['ctx'=8,'wt'=4] {'ctx'}, dimensions={1}, use_global_device_ids=true | all-gather | bytes 9216 | tf_op jit(solution)/shard_map/all_gather | solution.py:168
  62.1 146.0 %collective-permute-done.1 = bf16[2,512,2304]{2,1,0:T(8,128)(2,1)} collective-permute-done((bf16[2,512,2304]{2,1,0:T(8,128)(2,1)}, bf16[2,512,2304]{2,1,0:T(8,128)(2,1)}, u32[]{:S(2)}, u32[]{:S(2)}) %collective-permute-start.1) | collective-permute-done | bytes 4718624 | tf_op jit(solution)/shard_map/ppermute | solution.py:35
  208.2 8.3 pad_maximum_fusion
  216.5 12.3 %reverse_select_fusion = bf16[2,2,512,2304]{3,2,1,0:T(8,128)(2,1)} fusion(bf16[2,2,512,2304]{3,2,1,0:T(8,128)(2,1)} %pad_maximum_fusion, pred[]{:T(512)S(6)} %eq.73), kind=kLoop, calls=%fused_computation.68 | loop fusion | flops 4718592 | bytes 18874368 | tf_op jit(solution)/shard_map/jit(_where)/select_n | solution.py:39
  228.8 6.4 fusion.118
  238.7 33.4 %all_gather.25 = bf16[2048,128]{1,0:T(8,128)(2,1)} all-gather(bf16[256,128]{1,0:T(8,128)(2,1)S(1)} %fusion.115), channel_id=1, replica_groups=mesh['ctx'=8,'wt'=4] {'ctx'}, dimensions={0}, use_global_device_ids=true | all-gather | bytes 589824 | tf_op jit(solution)/shard_map/all_gather | solution.py:166
  272.4 5.0 while.39
  278.5 37.9 %all_gather.26 = bf16[2048,128]{1,0:T(8,128)(2,1)} all-gather(bf16[256,128]{1,0:T(8,128)(2,1)S(1)} %fusion.116), channel_id=1, replica_groups=mesh['ctx'=8,'wt'=4] {'ctx'}, dimensions={0}, use_global_device_ids=true | all-gather | bytes 589824 | tf_op jit(solution)/shard_map/all_gather | solution.py:167
  318.0 6.2 while.40
  318.3 5.9 fusion.282
  328.2 6.5 fusion.85
  340.1 12.4 %all-gather.8.cloned.1.call-done = bf16[2048,8192]{1,0:T(8,128)(2,1)} async-done(((bf16[512,8192]{1,0:T(8,128)(2,1)}), bf16[2048,8192]{1,0:T(8,128)(2,1)}) %all-gather.8.cloned.1.call-update) | async-done | bytes 33554448 | tf_op jit(solution)/shard_map/all_gather | solution.py:227
  352.6 22.3 %fusion.201 = f32[256,8192]{1,0:T(8,128)} fusion(bf16[256,2048]{1,0:T(8,128)(2,1)} %copy-done.19, bf16[2048,8192]{1,0:T(8,128)(2,1)} %all-gather.8.cloned.1.call-done), kind=kOutput, calls=%fused_computation.281 | convolution fusion | flops 8589934592 | bytes 42991616 | tf_op jit(solution)/shard_map/dot_general | solution.py:53
  374.9 10.4 multiply_convert_fusion
  385.3 170.4 %all-gather.10.cloned.1.call-done = bf16[8192,2048]{1,0:T(8,128)(2,1)} async-done(((bf16[2048,2048]{1,0:T(8,128)(2,1)}), bf16[8192,2048]{1,0:T(8,128)(2,1)}) %all-gather.10.cloned.1.call-update) | async-done | bytes 33554448 | tf_op jit(solution)/shard_map/all_gather | solution.py:232
  555.7 18.5 %fusion.124 = f32[256,8192]{1,0:T(8,128)} fusion(bf16[8192,2048]{1,0:T(8,128)(2,1)} %all-gather.10.cloned.1.call-done, bf16[1,256,2048]{2,1,0:T(8,128)(2,1)} %param.31), kind=kOutput, calls=%fused_computation.165 | convolution fusion | flops 8589934592 | bytes 42991616 | tf_op jit(solution)/shard_map/dot_general | solution.py:57
  574.2 23.2 %fusion.73 = bf16[256,8192]{1,0:T(8,128)(2,1)S(1)} fusion(f32[256,8192]{1,0:T(8,128)} %get-tuple-element.441, f32[256,8192]{1,0:T(8,128)} %fusion.124, bf16[16,256]{1,0:T(8,128)(2,1)S(1)} %convolution_convert_fusion.6, bf16[8,8192,16]{1,2,0:T(8,128)(2,1)} %param.52, s32[]{:T(128)S(6)} %select_n.102), kind=kOutput, calls=%fused_computation.79 | convolution fusion | flops 115343360 | bytes 21241860 | tf_op jit(solution)/shard_map/dot_general | solution.py:57
  600.6 17.0 %fusion.202 = f32[256,2048]{1,0:T(8,128)} fusion(bf16[256,8192]{1,0:T(8,128)(2,1)} %copy-done.13, bf16[2048,8192]{1,0:T(8,128)(2,1)} %all-gather.8.cloned.1.call-done), kind=kOutput, calls=%fused_computation.282 | convolution fusion | flops 8589934592 | bytes 39845888 | tf_op jit(solution)/shard_map/dot_general | solution.py:57
  617.6 2.6 fusion.198
  630.4 15.0 %while.41 = (s32[]{:T(128)}, f32[256,16,128]{2,0,1:T(8,128)S(1)}, f32[2048,128]{0,1:T(8,128)}, bf16[2048,128]{0,1:T(8,128)(2,1)}, s32[]{:T(128)}, /*index=5*/s32...) while((s32[]{:T(128)}, f32[256,16,128]{2,0,1:T(8,128)S(1)}, ...), condition=%wide.region_15.16_spmd.clone, body=%wide.region_14.15_spmd.clone.sunk | while | flops 2710438656 | bytes 55899472 | solution.py:288
  633.0 4.1 fusion.294
  637.1 2.6 convolution_add_fusion.13
  666.7 70.9 %reduce-scatter.5.cloned.1.call-done = bf16[256,128]{0,1:T(8,128)(2,1)} async-done(((bf16[2048,128]{0,1:T(8,128)(2,1)}), bf16[256,128]{0,1:T(8,128)(2,1)}) %reduce-scatter.5.cloned.1.call-update) | async-done | bytes 65552 | tf_op jit(solution)/shard_map/reduce_scatter | solution.py:295
  738.6 65.0 %reduce-scatter.3.cloned.1.call-done = bf16[256,128]{0,1:T(8,128)(2,1)} async-done(((bf16[2048,128]{0,1:T(8,128)(2,1)}), bf16[256,128]{0,1:T(8,128)(2,1)}) %reduce-scatter.3.cloned.1.call-update) | async-done | bytes 65552 | tf_op jit(solution)/shard_map/reduce_scatter | solution.py:292
  812.0 18.5 %convolution_add_fusion.9 = f32[256,2048]{1,0:T(8,128)S(1)} fusion(f32[256,2048]{1,0:T(8,128)S(1)} %copy-done.4, bf16[256,8192]{1,0:T(8,128)(2,1)} %get-tuple-element.440, bf16[8192,2048]{1,0:T(8,128)(2,1)} %all-gather.10.cloned.1.call-done), kind=kOutput, calls=%fused_computation.105 | convolution fusion | flops 8590458880 | bytes 41943040 | tf_op jit(solution)/shard_map/dot_general | solution.py:53
  832.9 35.3 %all-gather.12.cloned.1.call-done = bf16[2048,2304]{1,0:T(8,128)(2,1)} async-done(((bf16[512,2304]{1,0:T(8,128)(2,1)}), bf16[2048,2304]{1,0:T(8,128)(2,1)}) %all-gather.12.cloned.1.call-update) | async-done | bytes 9437200 | tf_op jit(solution)/shard_map/all_gather | solution.py:312
  868.2 5.2 fusion.109
  876.8 289.2 %all-reduce.3.cloned.1.call-done = (f32[8,2048,16]{1,2,0:T(8,128)}, f32[8,16,2048]{2,1,0:T(8,128)}, f32[8,2048,16]{1,2,0:T(8,128)}, f32[8,16,128]{2,1,0:T(8,128)...) async-done(((f32[8,2048,16]{1,2,0:T(8,128)}, ...) | async-done | bytes 16908304 | tf_op jit(solution)/shard_map/psum | solution.py:325
  (224 shorter events, 111.4 us)
Async XLA Ops:
  7.2 367.7 %copy-start = (bf16[8,16,8192]{2,1,0:T(8,128)(2,1)S(1)}, bf16[8,16,8192]{2,1,0:T(8,128)(2,1)}, u32[]{:S(2)}) copy-start(bf16[8,16,8192]{2,1,0:T(8,128)(2,1)} %param.51) | copy-start | bytes 6291460
  7.2 321.0 %all-gather.6.cloned.1.call-start = ((), (), s32[]{:S(2)}) async-start(), calls=%async_computation.2 | async-start | bytes 10485760 | tf_op jit(solution)/shard_map/all_gather | solution.py:221
  7.9 344.7 %all-gather.8.cloned.1.call-start = ((), (), s32[]{:S(2)}) async-start(), calls=%async_computation.3 | async-start | bytes 41943040 | tf_op jit(solution)/shard_map/all_gather | solution.py:227
  8.7 547.0 %all-gather.10.cloned.1.call-start = ((), (), s32[]{:S(2)}) async-start(), calls=%async_computation.4 | async-start | bytes 41943040 | tf_op jit(solution)/shard_map/all_gather | solution.py:232
  9.4 728.2 %reduce-scatter.5.cloned.1.call-start = ((), (), s32[]{:S(2)}) async-start(), calls=%async_computation.6 | async-start | bytes 589824 | tf_op jit(solution)/shard_map/reduce_scatter | solution.py:295
  9.5 5.1 collective-permute-start
  17.3 37.9 %copy-start.5 = (bf16[1,256,2048]{2,1,0:T(8,128)(2,1)S(1)}, bf16[1,256,2048]{2,1,0:T(8,128)(2,1)}, u32[]{:S(2)}) copy-start(bf16[1,256,2048]{2,1,0:T(8,128)(2,1)} %param.30) | copy-start | bytes 3145732
  22.8 37.4 %copy-start.40 = (f32[2048]{0:T(1024)S(1)}, f32[2048]{0:T(1024)}, u32[]{:S(2)}) copy-start(f32[2048]{0:T(1024)} %param.34) | copy-start | bytes 24580
  22.8 37.4 %copy-start.48 = (f32[2048]{0:T(1024)S(1)}, f32[2048]{0:T(1024)}, u32[]{:S(2)}) copy-start(f32[2048]{0:T(1024)} %param.35) | copy-start | bytes 24580
  22.8 185.4 %collective-permute-start.1 = (bf16[2,512,2304]{2,1,0:T(8,128)(2,1)}, bf16[2,512,2304]{2,1,0:T(8,128)(2,1)}, u32[]{:S(2)}, u32[]{:S(2)}) collective-permute-start(bf16[2,512,2304]{2,1,0:T(8,128)(2,1)} %get-tuple-element.424), channel_id=1, source_target_pairs={{0,2},{1,3},{2,0},{3,1},{4,6},{5,7},{6,4},{7,5},{8,10},{9,11},{10,... | collective-permute-start | bytes 14155784 | tf_op jit(solution)/shard_map/ppermute | solution.py:35
  55.5 173.3 %copy-start.44 = (f32[256]{0:T(256)}, f32[256]{0:T(256)S(1)}, u32[]{:S(2)}) copy-start(f32[256]{0:T(256)S(1)} %broadcast_multiply_fusion.17) | copy-start | bytes 3076
  55.9 172.8 %copy-start.46 = (f32[256]{0:T(256)}, f32[256]{0:T(256)S(1)}, u32[]{:S(2)}) copy-start(f32[256]{0:T(256)S(1)} %add_rsqrt_fusion.1) | copy-start | bytes 3076
  56.8 159.7 %copy-start.27 = (bf16[2048,16]{0,1:T(8,128)(2,1)}, bf16[2048,16]{0,1:T(8,128)(2,1)S(1)}, u32[]{:S(2)}) copy-start(bf16[2048,16]{0,1:T(8,128)(2,1)S(1)} %dynamic-slice_bitcast_fusion.2) | copy-start | bytes 196612
  57.7 158.8 %copy-start.29 = (bf16[2048,16]{0,1:T(8,128)(2,1)}, bf16[2048,16]{0,1:T(8,128)(2,1)S(1)}, u32[]{:S(2)}) copy-start(bf16[2048,16]{0,1:T(8,128)(2,1)S(1)} %get-tuple-element.444) | copy-start | bytes 196612
  62.1 215.3 %copy-start.35 = (bf16[256,48]{0,1:T(8,128)(2,1)}, bf16[256,48]{0,1:T(8,128)(2,1)S(1)}, u32[]{:S(2)}) copy-start(bf16[256,48]{0,1:T(8,128)(2,1)S(1)} %convolution_convert_fusion) | copy-start | bytes 73732
  235.2 37.2 %copy-start.22 = (f32[256,2304]{1,0:T(8,128)}, f32[256,2304]{1,0:T(8,128)S(1)}, u32[]{:S(2)}) copy-start(f32[256,2304]{1,0:T(8,128)S(1)} %fusion.118) | copy-start | bytes 7077892
  340.1 34.7 %copy-start.42 = (bf16[256,16]{0,1:T(8,128)(2,1)}, bf16[256,16]{0,1:T(8,128)(2,1)S(1)}, u32[]{:S(2)}) copy-start(bf16[256,16]{0,1:T(8,128)(2,1)S(1)} %convolution_convert_fusion.7) | copy-start | bytes 24580
  645.5 158.0 %reduce-scatter.3.cloned.1.call-start = ((), (), s32[]{:S(2)}) async-start(), calls=%async_computation.5 | async-start | bytes 589824 | tf_op jit(solution)/shard_map/reduce_scatter | solution.py:292
  647.7 220.5 %all-gather.12.cloned.1.call-start = ((), (), s32[]{:S(2)}) async-start(), calls=%async_computation.7 | async-start | bytes 11796480 | tf_op jit(solution)/shard_map/all_gather | solution.py:312
  648.3 517.8 %all-reduce.3.cloned.1.call-start = ((), (), s32[]{:S(2)}) async-start(), calls=%async_computation.8 | async-start | bytes 33816576 | tf_op jit(solution)/shard_map/psum | solution.py:325
  661.7 145.5 %copy-start.21 = (bf16[256,2048]{1,0:T(8,128)(2,1)S(1)}, bf16[256,2048]{1,0:T(8,128)(2,1)}, u32[]{:S(2)}) copy-start(bf16[256,2048]{1,0:T(8,128)(2,1)} %copy-done.20) | copy-start | bytes 3145732
  812.0 56.2 %copy-start.18 = (bf16[256,16,128]{0,2,1:T(8,128)(2,1)S(1)}, bf16[256,16,128]{0,2,1:T(8,128)(2,1)}, u32[]{:S(2)}) copy-start(bf16[256,16,128]{0,2,1:T(8,128)(2,1)} %copy-done.17) | copy-start | bytes 3145732
  812.0 56.2 %copy-start.33 = (bf16[256,128]{0,1:T(8,128)(2,1)S(1)}, bf16[256,128]{0,1:T(8,128)(2,1)}, u32[]{:S(2)}) copy-start(bf16[256,128]{0,1:T(8,128)(2,1)} %reduce-scatter.5.cloned.1.call-done) | copy-start | bytes 196612
  812.0 56.2 %copy-start.34 = (bf16[256,128]{0,1:T(8,128)(2,1)S(1)}, bf16[256,128]{0,1:T(8,128)(2,1)}, u32[]{:S(2)}) copy-start(bf16[256,128]{0,1:T(8,128)(2,1)} %reduce-scatter.3.cloned.1.call-done) | copy-start | bytes 196612
  832.8 40.6 %copy-start.6 = (bf16[1,256,2048]{2,1,0:T(8,128)(2,1)S(1)}, bf16[1,256,2048]{2,1,0:T(8,128)(2,1)}, u32[]{:S(2)}) copy-start(bf16[1,256,2048]{2,1,0:T(8,128)(2,1)} %param.30) | copy-start | bytes 3145732
  832.8 40.6 %copy-start.28 = (bf16[2048,16]{0,1:T(8,128)(2,1)S(1)}, bf16[2048,16]{0,1:T(8,128)(2,1)}, u32[]{:S(2)}) copy-start(bf16[2048,16]{0,1:T(8,128)(2,1)} %copy-done.27) | copy-start | bytes 196612
  832.8 40.6 %copy-start.30 = (bf16[2048,16]{0,1:T(8,128)(2,1)S(1)}, bf16[2048,16]{0,1:T(8,128)(2,1)}, u32[]{:S(2)}) copy-start(bf16[2048,16]{0,1:T(8,128)(2,1)} %copy-done.29) | copy-start | bytes 196612
  832.8 40.6 %copy-start.32 = (bf16[2048,16]{0,1:T(8,128)(2,1)S(1)}, bf16[2048,16]{0,1:T(8,128)(2,1)}, u32[]{:S(2)}) copy-start(bf16[2048,16]{0,1:T(8,128)(2,1)} %copy-done.31) | copy-start | bytes 196612
  832.8 40.6 %copy-start.41 = (f32[2048]{0:T(1024)S(1)}, f32[2048]{0:T(1024)}, u32[]{:S(2)}) copy-start(f32[2048]{0:T(1024)} %param.34) | copy-start | bytes 24580
  832.9 40.6 %copy-start.45 = (f32[256]{0:T(256)S(1)}, f32[256]{0:T(256)}, u32[]{:S(2)}) copy-start(f32[256]{0:T(256)} %copy-done.44) | copy-start | bytes 3076
  832.9 40.6 %copy-start.47 = (f32[256]{0:T(256)S(1)}, f32[256]{0:T(256)}, u32[]{:S(2)}) copy-start(f32[256]{0:T(256)} %copy-done.46) | copy-start | bytes 3076
  1166.1 21.2 %copy-start.1 = (bf16[8,16,8192]{2,1,0:T(8,128)(2,1)S(1)}, bf16[8,16,8192]{2,1,0:T(8,128)(2,1)}, u32[]{:S(2)}) copy-start(bf16[8,16,8192]{2,1,0:T(8,128)(2,1)} %param.51) | copy-start | bytes 6291460
  (29 other events, 113.0 us)
Sparse Core Ops, SparseCore 0:
  9.6 102.6 all-gather.5
  113.8 238.7 all-gather.7
  354.2 201.4 all-gather.9
  645.6 91.9 reduce-scatter.4
  741.3 62.1 reduce-scatter.2
  804.9 63.1 all-gather.11
  875.2 290.8 all-reduce.2
